TPU v7x, 128 devices: a whole 4x4x4 slice. The times are simulated.
128 devices in a mesh: seq: 4 (over x_lo, core), tensor: 32 (over z, y, x_hi).
Axes of the slice: x: 4 (x_hi: 2, x_lo: 2; x = x_hi * 2 + x_lo), y: 4, z: 4, core: 2. Of those that a mesh axis runs over, the one named last changes fastest.
Arguments:
- tokens: bfloat16 [2, 4096, 4096], P(None, 'seq', 'tensor'), may hold values from -6 to 6
- w_qkv: bfloat16 [4096, 3, 4096], P(None, None, 'tensor'), may hold values from -1 to 1
- q_gain: float32 [4096], P('tensor'), may hold values from 0.5 to 2.5
- k_gain: float32 [4096], P('tensor'), may hold values from 0.5 to 2.5
- w_out: bfloat16 [4096, 4096], P('tensor'), may hold values from -0.1875 to 0.1875
Outputs:
- mixed: bfloat16 [2, 4096, 4096], P(None, 'seq', 'tensor')
- peak: float32 [32], P('tensor')
- qk_scale: float32 [2, 2, 4096], P(None, None, 'seq')
All inputs are finite; a program needn't handle non-finite values.
Results may differ from a plain program's by a relative error of at most 0.024.
Values may be sent and summed in bfloat16 or wider, within the bound.
A program may use at most 128 MiB of HBM per device.

v0:
```python
import jax
import jax.numpy as jnp
from jax import lax
from jax.sharding import Mesh
from jax.sharding import PartitionSpec as P

HEADS = 32
TENSOR = ("tensor_0", "tensor_1", "tensor_2")
EPS = 1e-06
ROPE_BASE = 500000.0
NEG = -1e30


def sent_to_all(array, axis):
    size = lax.axis_size(axis)
    return lax.all_to_all(
        jnp.broadcast_to(array[None], (size, *array.shape)), axis, 0, 0, tiled=True
    )


def taken_together(array, axis):
    return sent_to_all(array, axis).sum(axis=0)


def side_by_side(arrays, axis, dim, along):
    both = jnp.concatenate(arrays, axis=along)
    filled, at, gathered = (lax.all_gather(both, axis, axis=dim, tiled=True), 0, [])
    for a in arrays:
        gathered.append(lax.slice_in_dim(filled, at, at + a.shape[along], axis=along))
        at += a.shape[along]
    return tuple(gathered)


def over_copies(array, axis):
    return sent_to_all(array, axis).max(axis=0)


def sum_by_axis(array, axes, dim):
    for axis in axes:
        array = lax.psum_scatter(array, axis, scatter_dimension=dim, tiled=True)
    return array


def rope_tables(positions, head):
    half = head // 2
    freq = ROPE_BASE ** (-(jnp.arange(half, dtype=jnp.float32) * 2.0) / head)
    angle = positions[:, None] * freq[None, :]
    return (jnp.cos(angle), jnp.sin(angle))


def rotate(values, cosine, sine):
    half = values.shape[-1] // 2
    first = values[..., :half]
    second = values[..., half:]
    cosine = cosine[:, None, :]
    sine = sine[:, None, :]
    return jnp.concatenate([first * cosine - second * sine, second * cosine + first * sine], -1)


def norm_stats(query, keyed, width):
    totals = taken_together(
        jnp.stack([jnp.sum(query * query, 1), jnp.sum(keyed * keyed, 1)]), TENSOR
    )
    return lax.rsqrt(totals / width + EPS)


def online_update(q_part, k_part, v_part, valid, state, scale):
    top, denom, accum = state
    scores = jnp.einsum("sqd,skd->sqk", q_part, k_part, preferred_element_type=jnp.float32) * scale
    scores = jnp.where(valid[None], scores, NEG)
    new_top = jnp.maximum(top, jnp.max(scores, -1))
    weights = jnp.where(valid[None], jnp.exp(scores - new_top[..., None]), 0.0)
    factor = jnp.exp(top - new_top)
    added = jnp.einsum(
        "sqk,skd->sqd", weights.astype(jnp.bfloat16), v_part, preferred_element_type=jnp.float32
    )
    return (new_top, denom * factor + jnp.sum(weights, -1), accum * factor[..., None] + added)


def shards(tokens, w_qkv, q_gain, k_gain, w_out):
    seqs, tok, dloc = tokens.shape
    width = w_qkv.shape[0]
    head = width // HEADS
    heads_here = dloc // head
    rows = seqs * tok
    flat_w = w_qkv.reshape(width, 3 * dloc)
    whole = lax.all_gather(tokens, TENSOR, axis=2, tiled=True).reshape(rows, width)
    paired = jnp.dot(whole, flat_w[:, : 2 * dloc], preferred_element_type=jnp.float32)
    query = paired[:, :dloc]
    keyed = paired[:, dloc:]
    inverse = norm_stats(query, keyed, width)
    value = jnp.dot(whole, flat_w[:, 2 * dloc :], preferred_element_type=jnp.float32)
    own_index = lax.axis_index("seq")
    q_index = own_index * tok + jnp.arange(tok, dtype=jnp.int32)
    cosine, sine = rope_tables(q_index.astype(jnp.float32), head)

    def prepare(projection, scale_row, gain):
        normed = projection * scale_row[:, None] * gain[None, :]
        return rotate(normed.reshape(seqs, tok, heads_here, head), cosine, sine).astype(
            jnp.bfloat16
        )

    q_heads = prepare(query, inverse[0], q_gain).transpose(2, 0, 1, 3)
    k_ready = prepare(keyed, inverse[1], k_gain).reshape(seqs, tok, dloc)
    v_ready = value.astype(jnp.bfloat16).reshape(seqs, tok, dloc)
    scale = head ** (-0.5)
    keys_all, values_all = side_by_side((k_ready, v_ready), "seq", 1, 0)
    total_len = keys_all.shape[1]
    k_heads = keys_all.reshape(seqs, total_len, heads_here, head).transpose(2, 0, 1, 3)
    v_heads = values_all.reshape(seqs, total_len, heads_here, head).transpose(2, 0, 1, 3)

    def attend(operands):
        q_one, k_one, v_one = operands

        def visit(step, state):
            first = step * tok
            k_part = lax.dynamic_slice_in_dim(k_one, first, tok, 1)
            v_part = lax.dynamic_slice_in_dim(v_one, first, tok, 1)
            valid = (first + jnp.arange(tok, dtype=jnp.int32))[None, :] <= q_index[:, None]
            return online_update(q_one, k_part, v_part, valid, state, scale)

        initial = (
            jnp.full((seqs, tok), NEG, jnp.float32),
            jnp.zeros((seqs, tok), jnp.float32),
            jnp.zeros((seqs, tok, head), jnp.float32),
        )
        top, denom, accum = lax.fori_loop(0, own_index + 1, visit, initial)
        return (accum / denom[..., None], top)

    outputs, tops = lax.map(attend, (q_heads, k_heads, v_heads))
    attended = outputs.astype(jnp.bfloat16).transpose(1, 2, 0, 3).reshape(rows, dloc)
    peak = over_copies(jnp.max(tops, axis=(1, 2)), "seq")
    partial_out = (
        jnp.dot(attended, w_out, preferred_element_type=jnp.float32)
        .astype(jnp.bfloat16)
        .reshape(seqs, tok, width)
    )
    mixed = sum_by_axis(partial_out, TENSOR, 2).astype(jnp.float32)
    return (mixed.astype(jnp.bfloat16), peak, inverse.reshape(2, seqs, tok))


def solution(mesh):
    finer = Mesh(
        mesh.devices.reshape(mesh.shape["seq"], 4, 4, 2),
        ("seq", "tensor_0", "tensor_1", "tensor_2"),
    )
    placed = (P(None, "seq", TENSOR), P(None, None, TENSOR), P(TENSOR), P(TENSOR), P(TENSOR, None))
    return jax.shard_map(
        shards,
        mesh=finer,
        in_specs=placed,
        out_specs=(P(None, "seq", TENSOR), P(TENSOR), P(None, None, "seq")),
        check_vma=False,
    )
```

profile of v0, /device:TPU:1, one launch (start us, length us, event | category | flops | bytes accessed | tf_op | source)
XLA Modules:
  0.0 593.4 jit_solution(10021887254225840839)
XLA Ops:
  7.2 0.0 copy-start
  7.2 0.0 all-gather.3.cloned.1.call-start
  7.2 0.7 all-gather.3.cloned.1.call-update
  7.9 4.7 copy.16
  12.7 3.1 multiply_cosine_fusion
  15.7 205.0 %all-gather.3.cloned.1.call-done = bf16[2,1024,4096]{2,1,0:T(8,128)(2,1)} async-done(((bf16[2,1024,128]{2,1,0:T(8,128)(2,1)}), bf16[2,1024,4096]{2,1,0:T(8,128)(2,1)}) %all-gather.3.cloned.1.call-update) | async-done | bytes 16777232 | tf_op jit(solution)/shard_map/all_gather | solution.py:87
  220.7 8.8 %fusion.19 = f32[2048,256]{1,0:T(8,128)S(1)} fusion(bf16[2048,4096]{1,0:T(8,128)(2,1)} %bitcast.64, bf16[4096,384]{0,1:T(8,128)(2,1)} %bitcast.55), kind=kOutput, calls=%fused_computation.24 | convolution fusion | flops 4294967296 | bytes 20971520 | tf_op jit(solution)/shard_map/dot_general | solution.py:88
  229.5 0.6 multiply_reduce_fusion.1
  230.1 1.0 broadcast_in_dim.36
  231.2 5.4 all-to-all-start
  236.6 0.0 copy-start.2
  236.6 0.0 copy-start.3
  236.6 0.0 all-gather.5.cloned.1.call-start
  236.7 11.3 %convolution_convert_fusion.1 = bf16[2048,128]{1,0:T(8,128)(2,1)} fusion(bf16[2048,4096]{1,0:T(8,128)(2,1)} %bitcast.65, bf16[4096,384]{0,1:T(8,128)(2,1)} %bitcast.56), kind=kOutput, calls=%fused_computation.23 | convolution fusion | flops 2147745792 | bytes 18350080 | tf_op jit(solution)/shard_map/dot_general | solution.py:92
  248.0 0.5 all-to-all-done
  248.5 1.2 reduce_sum.38
  249.8 0.0 copy-start.1
  249.8 0.0 copy-done.2
  249.8 0.0 copy-done.3
  249.8 0.7 multiply_multiply_fusion
  250.6 2.0 fusion.24
  252.5 0.0 copy-done.1
  252.5 1.3 pad_maximum_fusion
  253.8 0.0 all-gather.5.cloned.1.call-update
  253.8 0.2 reduce-scatter.6.cloned.1.call-start
  254.1 1.1 pad_maximum_fusion.1
  255.1 48.1 %all-gather.5.cloned.1.call-done = bf16[4,4096,128]{2,1,0:T(8,128)(2,1)} async-done(((bf16[4,1024,128]{2,1,0:T(8,128)(2,1)}), bf16[4,4096,128]{2,1,0:T(8,128)(2,1)}) %all-gather.5.cloned.1.call-update) | async-done | bytes 4194320 | tf_op jit(solution)/shard_map/all_gather | solution.py:27
  303.3 4.5 fusion.26
  307.7 0.1 broadcast.114
  307.8 21.6 %while.25 = (s32[]{:T(128)}, f32[2,1024]{1,0:T(2,128)S(1)}, f32[2,1024]{1,0:T(2,128)S(1)}, f32[2,1024,128]{2,1,0:T(8,128)S(1)}, s32[]{:T(128)}, /*index=5*/bf16[...) while((s32[]{:T(128)}, f32[2,1024]{1,0:T(2,128)S(1)}, ...), condition=%wide.region_6.7_spmd.clone, body=%wide.region_3.6_spmd.clone.sunk | while | flops 1102583808 | bytes 33177796 | solution.py:127
  307.8 0.7 broadcast_compare_fusion.2
  308.5 3.0 fusion.42
  311.5 2.3 fusion.43
  313.8 4.8 fusion.44
  318.6 0.7 broadcast_compare_fusion.2
  319.3 3.0 fusion.42
  322.3 2.3 fusion.43
  324.6 4.8 fusion.44
  329.4 0.3 divide_convert_fusion
  329.7 0.0 copy-done
  329.7 8.0 %convolution_convert_fusion = bf16[2048,4096]{1,0:T(8,128)(2,1)} fusion(bf16[2048,128]{1,0:T(8,128)(2,1)S(1)} %bitcast.57, bf16[128,4096]{1,0:T(8,128)(2,1)S(1)} %copy-done), kind=kOutput, calls=%fused_computation.22 | convolution fusion | flops 2155872256 | bytes 18350080 | tf_op jit(solution)/shard_map/dot_general | solution.py:134
  337.8 0.0 reduce-scatter.6.cloned.1.call-update
  337.8 0.0 reduce-scatter.8.cloned.1.call-start
  337.9 169.6 %reduce-scatter.6.cloned.1.call-done = bf16[2,1024,1024]{2,1,0:T(8,128)(2,1)} async-done(((bf16[2,1024,4096]{2,1,0:T(8,128)(2,1)}), bf16[2,1024,1024]{2,1,0:T(8,128)(2,1)}) %reduce-scatter.6.cloned.1.call-update) | async-done | bytes 4194320 | tf_op jit(solution)/shard_map/reduce_scatter | solution.py:40
  507.5 0.0 reduce-scatter.8.cloned.1.call-update
  507.5 0.0 reduce-scatter.10.cloned.1.call-start
  507.6 48.6 %reduce-scatter.8.cloned.1.call-done = bf16[2,1024,256]{2,1,0:T(8,128)(2,1)} async-done(((bf16[2,1024,1024]{2,1,0:T(8,128)(2,1)}), bf16[2,1024,256]{2,1,0:T(8,128)(2,1)}) %reduce-scatter.8.cloned.1.call-update) | async-done | bytes 1048592 | tf_op jit(solution)/shard_map/reduce_scatter | solution.py:40
  556.2 2.6 copy.20
  558.8 1.3 copy.24
  560.0 0.0 reduce-scatter.10.cloned.1.call-update
  560.1 0.6 rsqrt.8
  560.7 0.6 reduce_max.29
  561.3 0.6 broadcast_in_dim.37
  562.0 6.4 %all_to_all.11 = f32[4,1,1]{2,1,0:T(1,128)S(1)} all-to-all(f32[4,1,1]{2,1,0:T(1,128)S(1)} %broadcast_in_dim.37), channel_id=1, replica_groups=mesh['seq'=4,'tensor_0'=4,'tensor_1'=4,'tensor_2'=2] {'seq'}, dimensions={0} | all-to-all | bytes 32 | tf_op jit(solution)/shard_map/all_to_all | solution.py:16
  568.3 0.6 reduce_max.30
  568.9 15.3 %reduce-scatter.10.cloned.1.call-done = bf16[128,2048]{1,0:T(8,128)(2,1)} async-done(((bf16[256,2048]{1,0:T(8,128)(2,1)}), bf16[128,2048]{1,0:T(8,128)(2,1)}) %reduce-scatter.10.cloned.1.call-update) | async-done | bytes 524304
  584.2 1.4 reshape.187
  585.7 1.2 copy.21
  (15 shorter events, 0.1 us)
Async XLA Ops:
  7.2 322.6 %copy-start = (bf16[128,4096]{1,0:T(8,128)(2,1)S(1)}, bf16[128,4096]{1,0:T(8,128)(2,1)}, u32[]{:S(2)}) copy-start(bf16[128,4096]{1,0:T(8,128)(2,1)} %param.11) | copy-start | bytes 3145732
  7.2 213.6 %all-gather.3.cloned.1.call-start = ((), (), s32[]{:S(2)}) async-start(), calls=%async_computation.5 | async-start | bytes 17301504 | tf_op jit(solution)/shard_map/all_gather | solution.py:87
  231.2 17.4 %all-to-all-start = ((f32[32,2,2048]{2,1,0:T(2,128)}), f32[32,2,2048]{2,1,0:T(2,128)}, u32[]{:S(2)}, u32[]{:S(2)}) async-start(f32[32,2,2048]{2,1,0:T(2,128)} %broadcast_in_dim.36), calls=%async_computation | async-start | bytes 1048576 | tf_op jit(solution)/shard_map/all_to_all | solution.py:16
  236.6 13.2 %copy-start.2 = (f32[128]{0:T(128)S(1)}, f32[128]{0:T(128)}, u32[]{:S(2)}) copy-start(f32[128]{0:T(128)} %param.9) | copy-start | bytes 1540
  236.6 13.2 %copy-start.3 = (f32[128]{0:T(128)S(1)}, f32[128]{0:T(128)}, u32[]{:S(2)}) copy-start(f32[128]{0:T(128)} %param.10) | copy-start | bytes 1540
  236.6 66.6 %all-gather.5.cloned.1.call-start = ((), (), s32[]{:S(2)}) async-start(), calls=%async_computation.6 | async-start | bytes 5242880 | tf_op jit(solution)/shard_map/all_gather | solution.py:27
  249.8 2.8 copy-start.1
  253.8 253.7 %reduce-scatter.6.cloned.1.call-start = ((), (), s32[]{:S(2)}) async-start(), calls=%async_computation.7 | async-start | bytes 20971520 | tf_op jit(solution)/shard_map/reduce_scatter | solution.py:40
  337.8 218.4 %reduce-scatter.8.cloned.1.call-start = ((), (), s32[]{:S(2)}) async-start(), calls=%async_computation.8 | async-start | bytes 5242880 | tf_op jit(solution)/shard_map/reduce_scatter | solution.py:40
  507.5 76.7 %reduce-scatter.10.cloned.1.call-start = ((), (), s32[]{:S(2)}) async-start(), calls=%async_computation.9 | async-start | bytes 1572864
Sparse Core Ops, SparseCore 0:
  10.7 209.9 all-gather.2
  253.9 49.2 all-gather.4
  337.9 169.4 reduce-scatter.5
  509.7 46.4 reduce-scatter.7
  560.2 24.0 reduce-scatter.9
where the time goes:
time: 594 us; the launch traced here: 593 us
  waiting for transfers between devices  488 us (82%)
  matrix products  43.7 us (7%)
  local copies, waits for them, and re-layouts  18.1 us (3%)
  other arithmetic  17.4 us (3%)
  between operations  14 us (2%)
  blocking collectives  6.36 us (1%)
    reduce_scatter x2, waiting for transfers between devices, sum_by_axis(): array = lax.psum_scatter(array, axis, scatter_dimension=dim, tiled=True)  218 us
    all_gather x1, waiting for transfers between devices, shards(): lax.all_gather(tokens, TENSOR, axis=2, tiled=True).reshape(rows, width)  205 us
    all_gather x1, waiting for transfers between devices, side_by_side(): lax.all_gather(both, axis, axis=dim, tiled=True)  48.1 us
    unnamed x6, waiting for transfers between devices  16.1 us
  transfers between devices with their start and end apart: 6, of which 6 were waited for; matrix products, arithmetic and copies ran while one was open for 4% of the time, Pallas kernels for 0%

commit v1 on v0

--- a/solution.py
+++ b/solution.py
@@ -84,7 +84,7 @@
     heads_here = dloc // head
     rows = seqs * tok
     flat_w = w_qkv.reshape(width, 3 * dloc)
-    whole = lax.all_gather(tokens, TENSOR, axis=2, tiled=True).reshape(rows, width)
+    whole = jnp.concatenate(lax.all_gather(tokens, TENSOR), axis=2).reshape(rows, width)
     paired = jnp.dot(whole, flat_w[:, : 2 * dloc], preferred_element_type=jnp.float32)
     query = paired[:, :dloc]
     keyed = paired[:, dloc:]

time: 594 us -> 567 us (0.955)
  waiting for transfers between devices: 488 us -> 437 us
  local copies, waits for them, and re-layouts: 18.1 us -> 36.8 us
    all_gather x1, waiting for transfers between devices: 205 us -> 154 us  [shards(): lax.all_gather(tokens, TENSOR)]
    all_gather x0 -> x1, local copies, waits for them, and re-layouts: none -> 18.7 us  [shards(): lax.all_gather(tokens, TENSOR)]
  transfers between devices with their start and end apart: 6 -> 6, of which waited for: 6 -> 5; matrix products, arithmetic and copies ran while one was open for 4% -> 4% of each run, Pallas kernels for 0% -> 0%
where the time goes in v1:
time: 567 us; the launch traced here: 566 us
  waiting for transfers between devices  437 us (77%)
  matrix products  48.4 us (9%)
  local copies, waits for them, and re-layouts  36.8 us (6%)
  other arithmetic  17.4 us (3%)
  between operations  14 us (2%)
  blocking collectives  6.34 us (1%)
  starting transfers between devices  6.18 us (1%)
    reduce_scatter x2, waiting for transfers between devices, sum_by_axis(): array = lax.psum_scatter(array, axis, scatter_dimension=dim, tiled=True)  218 us
    all_gather x1, waiting for transfers between devices, shards(): lax.all_gather(tokens, TENSOR)  154 us
    all_gather x1, waiting for transfers between devices, side_by_side(): lax.all_gather(both, axis, axis=dim, tiled=True)  48.6 us
    all_gather x1, local copies, waits for them, and re-layouts, shards(): lax.all_gather(tokens, TENSOR)  18.7 us
    unnamed x6, waiting for transfers between devices  16 us
    dot_general x1, matrix products, shards(): jnp.dot(whole, flat_w[:, 2 * dloc:], preferred_element_type=jnp.float32)  12.4 us
    dot_general x1, matrix products, shards(): jnp.dot(whole, flat_w[:, :2 * dloc], preferred_element_type=jnp.float32)  12.4 us
  transfers between devices with their start and end apart: 6, of which 5 were waited for; matrix products, arithmetic and copies ran while one was open for 4% of the time, Pallas kernels for 0%

profile of v1, /device:TPU:1, one launch (start us, length us, event | category | flops | bytes accessed | tf_op | source)
XLA Modules:
  0.0 566.2 jit_solution(7591308062400247604)
XLA Ops:
  7.2 0.0 copy-start
  7.2 0.0 all-gather.6.cloned.1.call-start
  7.2 0.7 all-gather.6.cloned.1.call-update
  7.9 4.7 copy.20
  12.7 3.1 multiply_cosine_fusion
  15.7 154.0 %all-gather.6.cloned.1.call-done = bf16[64,1024,128]{2,1,0:T(8,128)(2,1)} async-done(((bf16[2,1024,128]{2,1,0:T(8,128)(2,1)}), bf16[64,1024,128]{2,1,0:T(8,128)(2,1)}) %all-gather.6.cloned.1.call-update) | async-done | bytes 16777232 | tf_op jit(solution)/shard_map/all_gather | solution.py:87
  169.7 0.0 copy-start.1
  169.7 18.7 %copy.19 = bf16[32,2,1024,128]{3,0,2,1:T(8,128)(2,1)} copy(bf16[32,2,1024,128]{3,2,1,0:T(8,128)(2,1)} %bitcast.59) | data formatting | bytes 33554432 | tf_op jit(solution)/shard_map/all_gather | solution.py:87
  188.4 0.0 copy-done.1
  188.4 12.4 %fusion.21 = f32[2048,256]{1,0:T(8,128)S(1)} fusion(bf16[256,8,32,128]{3,2,1,0:T(8,128)(2,1)} %bitcast.60, bf16[4096,384]{0,1:T(8,128)(2,1)S(1)} %bitcast.67), kind=kOutput, calls=%fused_computation.24 | convolution fusion | flops 4294967296 | bytes 20971520 | tf_op jit(solution)/shard_map/dot_general | solution.py:88
  200.8 0.6 multiply_reduce_fusion.1
  201.4 1.0 broadcast_in_dim.36
  202.5 5.6 all-to-all-start
  208.1 0.0 copy-start.3
  208.1 0.0 copy-start.4
  208.1 0.2 all-gather.4.cloned.1.call-start
  208.3 12.4 %fusion.25 = bf16[2048,128]{1,0:T(8,128)(2,1)} fusion(bf16[256,8,32,128]{3,2,1,0:T(8,128)(2,1)} %bitcast.61, bf16[4096,384]{0,1:T(8,128)(2,1)} %bitcast.66), kind=kOutput, calls=%fused_computation.29 | convolution fusion | flops 2147745792 | bytes 18350080 | tf_op jit(solution)/shard_map/dot_general | solution.py:92
  220.7 0.0 all-to-all-done
  220.7 1.2 reduce_sum.38
  221.9 0.0 copy-start.2
  222.0 0.0 copy-done.3
  222.0 0.0 copy-done.4
  222.0 0.7 multiply_multiply_fusion
  222.7 2.0 fusion.32
  224.7 0.0 copy-done.2
  224.7 1.3 pad_maximum_fusion
  225.9 0.0 all-gather.4.cloned.1.call-update
  226.0 0.3 reduce-scatter.6.cloned.1.call-start
  226.2 1.1 pad_maximum_fusion.1
  227.3 48.6 %all-gather.4.cloned.1.call-done = bf16[4,4096,128]{2,1,0:T(8,128)(2,1)} async-done(((bf16[4,1024,128]{2,1,0:T(8,128)(2,1)}), bf16[4,4096,128]{2,1,0:T(8,128)(2,1)}) %all-gather.4.cloned.1.call-update) | async-done | bytes 4194320 | tf_op jit(solution)/shard_map/all_gather | solution.py:27
  275.9 4.5 fusion.34
  280.4 0.1 broadcast.114
  280.5 21.6 %while.25 = (s32[]{:T(128)}, f32[2,1024]{1,0:T(2,128)S(1)}, f32[2,1024]{1,0:T(2,128)S(1)}, f32[2,1024,128]{2,1,0:T(8,128)S(1)}, s32[]{:T(128)}, /*index=5*/bf16[...) while((s32[]{:T(128)}, f32[2,1024]{1,0:T(2,128)S(1)}, ...), condition=%wide.region_6.7_spmd.clone, body=%wide.region_3.6_spmd.clone.sunk | while | flops 1102583808 | bytes 33177788 | solution.py:127
  280.5 0.7 broadcast_compare_fusion.2
  281.2 3.0 fusion.48
  284.2 2.3 fusion.49
  286.5 4.8 fusion.50
  291.3 0.7 broadcast_compare_fusion.2
  292.0 3.0 fusion.48
  295.0 2.3 fusion.49
  297.3 4.8 fusion.50
  302.1 0.3 divide_convert_fusion
  302.4 0.0 copy-done
  302.4 8.2 %convolution_convert_fusion = bf16[2048,4096]{1,0:T(8,128)(2,1)} fusion(bf16[2048,128]{1,0:T(8,128)(2,1)S(1)} %bitcast.68, bf16[128,4096]{1,0:T(8,128)(2,1)S(1)} %copy-done), kind=kOutput, calls=%fused_computation.26 | convolution fusion | flops 2155872256 | bytes 18350080 | tf_op jit(solution)/shard_map/dot_general | solution.py:134
  310.6 0.0 reduce-scatter.6.cloned.1.call-update
  310.6 0.0 reduce-scatter.8.cloned.1.call-start
  310.7 169.6 %reduce-scatter.6.cloned.1.call-done = bf16[2,1024,1024]{2,1,0:T(8,128)(2,1)} async-done(((bf16[2,1024,4096]{2,1,0:T(8,128)(2,1)}), bf16[2,1024,1024]{2,1,0:T(8,128)(2,1)}) %reduce-scatter.6.cloned.1.call-update) | async-done | bytes 4194320 | tf_op jit(solution)/shard_map/reduce_scatter | solution.py:40
  480.3 0.0 reduce-scatter.8.cloned.1.call-update
  480.3 0.0 reduce-scatter.10.cloned.1.call-start
  480.4 48.7 %reduce-scatter.8.cloned.1.call-done = bf16[2,1024,256]{2,1,0:T(8,128)(2,1)} async-done(((bf16[2,1024,1024]{2,1,0:T(8,128)(2,1)}), bf16[2,1024,256]{2,1,0:T(8,128)(2,1)}) %reduce-scatter.8.cloned.1.call-update) | async-done | bytes 1048592 | tf_op jit(solution)/shard_map/reduce_scatter | solution.py:40
  529.0 2.6 copy.24
  531.6 1.3 copy.29
  532.9 0.0 reduce-scatter.10.cloned.1.call-update
  532.9 0.6 rsqrt.8
  533.5 0.6 reduce_max.29
  534.2 0.6 broadcast_in_dim.37
  534.8 6.3 %all_to_all.11 = f32[4,1,1]{2,1,0:T(1,128)S(1)} all-to-all(f32[4,1,1]{2,1,0:T(1,128)S(1)} %broadcast_in_dim.37), channel_id=1, replica_groups=mesh['seq'=4,'tensor_0'=4,'tensor_1'=4,'tensor_2'=2] {'seq'}, dimensions={0} | all-to-all | bytes 32 | tf_op jit(solution)/shard_map/all_to_all | solution.py:16
  541.2 0.6 reduce_max.30
  541.8 15.3 %reduce-scatter.10.cloned.1.call-done = bf16[128,2048]{1,0:T(8,128)(2,1)} async-done(((bf16[256,2048]{1,0:T(8,128)(2,1)}), bf16[128,2048]{1,0:T(8,128)(2,1)}) %reduce-scatter.10.cloned.1.call-update) | async-done | bytes 524304
  557.1 1.4 reshape.188
  558.5 1.2 copy.25
  (15 shorter events, 0.2 us)
Async XLA Ops:
  7.2 295.3 %copy-start = (bf16[128,4096]{1,0:T(8,128)(2,1)S(1)}, bf16[128,4096]{1,0:T(8,128)(2,1)}, u32[]{:S(2)}) copy-start(bf16[128,4096]{1,0:T(8,128)(2,1)} %param.11) | copy-start | bytes 3145732
  7.2 162.5 %all-gather.6.cloned.1.call-start = ((), (), s32[]{:S(2)}) async-start(), calls=%async_computation.8 | async-start | bytes 17301504 | tf_op jit(solution)/shard_map/all_gather | solution.py:87
  169.7 18.7 %copy-start.1 = (bf16[4096,3,128]{0,2,1:T(8,128)(2,1)S(1)}, bf16[4096,3,128]{0,2,1:T(8,128)(2,1)}, u32[]{:S(2)}) copy-start(bf16[4096,3,128]{0,2,1:T(8,128)(2,1)} %copy.20) | copy-start | bytes 9437188
  202.5 18.2 %all-to-all-start = ((f32[32,2,2048]{2,1,0:T(2,128)}), f32[32,2,2048]{2,1,0:T(2,128)}, u32[]{:S(2)}, u32[]{:S(2)}) async-start(f32[32,2,2048]{2,1,0:T(2,128)} %broadcast_in_dim.36), calls=%async_computation | async-start | bytes 1048576 | tf_op jit(solution)/shard_map/all_to_all | solution.py:16
  208.1 13.9 %copy-start.3 = (f32[128]{0:T(128)S(1)}, f32[128]{0:T(128)}, u32[]{:S(2)}) copy-start(f32[128]{0:T(128)} %param.9) | copy-start | bytes 1540
  208.1 13.9 %copy-start.4 = (f32[128]{0:T(128)S(1)}, f32[128]{0:T(128)}, u32[]{:S(2)}) copy-start(f32[128]{0:T(128)} %param.10) | copy-start | bytes 1540
  208.1 67.8 %all-gather.4.cloned.1.call-start = ((), (), s32[]{:S(2)}) async-start(), calls=%async_computation.5 | async-start | bytes 5242880 | tf_op jit(solution)/shard_map/all_gather | solution.py:27
  221.9 2.8 copy-start.2
  226.0 254.3 %reduce-scatter.6.cloned.1.call-start = ((), (), s32[]{:S(2)}) async-start(), calls=%async_computation.6 | async-start | bytes 20971520 | tf_op jit(solution)/shard_map/reduce_scatter | solution.py:40
  310.6 218.4 %reduce-scatter.8.cloned.1.call-start = ((), (), s32[]{:S(2)}) async-start(), calls=%async_computation.7 | async-start | bytes 5242880 | tf_op jit(solution)/shard_map/reduce_scatter | solution.py:40
  480.3 76.7 %reduce-scatter.10.cloned.1.call-start = ((), (), s32[]{:S(2)}) async-start(), calls=%async_computation.9 | async-start | bytes 1572864
Sparse Core Ops, SparseCore 0:
  11.1 158.5 all-gather.5
  226.1 49.8 all-gather.3
  310.8 169.4 reduce-scatter.5
  482.6 46.4 reduce-scatter.7
  533.0 23.9 reduce-scatter.9
